TPU v7x, 32 devices: a whole 2x2x4 slice. The times are simulated.
32 devices in a mesh: seq: 8 (over z, x), head: 4 (over y, core).
Axes of the slice: x: 2, y: 2, z: 4, core: 2. Of those that a mesh axis runs over, the one named last changes fastest.
Arguments:
- tokens: bfloat16 [2048, 4608], P('seq', 'head'), may hold values from -32 to 32
- segments: int32 [2048], P('seq'), may hold values from 0 to 7, never falling along the last dimension, each value on 1 to 1024 neighbouring positions
- pre_gain: float32 [4608], replicated, may hold values from 0.1 to 1.9
- post_gain: float32 [4608], replicated, may hold values from 0.1 to 1.9
- w_query: bfloat16 [4608, 1024], P('seq', 'head'), may hold values from -0.375 to 0.375
- w_key: bfloat16 [4608, 512], P('seq', 'head'), may hold values from -0.1875 to 0.1875
- w_value: bfloat16 [4608, 512], P('seq', 'head'), may hold values from -0.09375 to 0.09375
- w_out: bfloat16 [1024, 4608], P('head', 'seq'), may hold values from -0.1875 to 0.1875
Outputs:
- mixed: bfloat16 [2048, 4608], P('seq')
Inputs may be any that keep to these rules, and one draw needn't show every extreme that they name: `segments`: segment ids never fall; each of the 8 documents holds at least one token and at most 1024, one exactly 1024.
All inputs are finite; a program needn't handle non-finite values.
Results may differ from a plain program's by a relative error of at most 0.01.
Values may be sent and summed in bfloat16 or wider, within the bound.
A program may use at most 64 MiB of HBM per device.

v0:
```python
import jax
import jax.numpy as jnp
from jax import lax
from jax.sharding import PartitionSpec as P

HD = 128
GROUP = 2
SCALAR = 144
DOCS = 8
EPS = 1e-06
CAP = 50.0


def carried_in(value, axis, join, neutral):
    count, mine = (lax.axis_size(axis), lax.axis_index(axis))
    pieces = lax.all_gather(value, axis)
    subtotal = jnp.full_like(value, 0) + jnp.asarray(neutral, value.dtype)

    def step(position, subtotal):
        longer = join(subtotal, pieces[position])
        return jnp.where(position < mine, longer, subtotal)

    return lax.fori_loop(0, count - 1, step, subtotal)


def rotate(values, position, width):
    count = values.shape[1] // width
    half = width // 2
    shaped = values.reshape(values.shape[0], count, width)
    freq = 10000.0 ** (-(jnp.arange(half, dtype=jnp.float32) / half))
    angle = position[:, None] * freq[None, :]
    cosine = jnp.cos(angle)[:, None, :]
    sine = jnp.sin(angle)[:, None, :]
    first = shaped[:, :, :half]
    second = shaped[:, :, half:]
    turned = jnp.concatenate(
        [first * cosine - second * sine, second * cosine + first * sine], axis=2
    )
    return turned.reshape(values.shape[0], count * width)


def add_counts(earlier, later):
    return earlier + later


def local(tokens, segments, pre_gain, post_gain, w_query, w_key, w_value, w_out):
    rows = tokens.shape[0]
    whole = lax.all_gather(tokens, "head", axis=1, tiled=True)
    wide = whole.astype(jnp.float32)
    normed = (
        wide * lax.rsqrt(jnp.mean(wide * wide, axis=1, keepdims=True) + EPS) * pre_gain
    ).astype(jnp.bfloat16)
    pieces = (
        lax.all_gather(w_query, "seq", axis=0, tiled=True),
        lax.all_gather(w_key, "seq", axis=0, tiled=True),
        lax.all_gather(w_value, "seq", axis=0, tiled=True),
    )
    query, key_proj, value_proj = tuple(
        (jnp.dot(normed, piece, preferred_element_type=jnp.float32) for piece in pieces)
    )
    levels = jnp.arange(DOCS, dtype=jnp.int32)
    below = jnp.sum((levels[None, :] > segments[:, None]).astype(jnp.float32), axis=0)
    earlier = carried_in(below, "seq", add_counts, jnp.zeros((DOCS,), jnp.float32))
    starts = earlier + below
    onehot = (segments[:, None] == levels[None, :]).astype(jnp.float32)
    tok_start = jnp.sum(onehot * starts[None, :], axis=1)
    offset = lax.axis_index("seq") * rows
    index_f = (offset + jnp.arange(rows, dtype=jnp.int32)).astype(jnp.float32)
    position = index_f - tok_start
    kv_count = w_key.shape[1] // HD
    rq = (rotate(query, position, HD) * SCALAR ** (-0.5)).astype(jnp.bfloat16)
    rk = rotate(key_proj, position, HD).astype(jnp.bfloat16)
    vb = value_proj.astype(jnp.bfloat16)
    stacked = (
        rq.reshape(rows, kv_count, GROUP, HD)
        .transpose(1, 2, 0, 3)
        .reshape(kv_count, GROUP * rows, HD)
    )
    query_start = jnp.tile(tok_start, GROUP)
    query_index = jnp.tile(index_f, GROUP)
    empty = (
        jnp.zeros((kv_count, GROUP * rows, HD), jnp.float32),
        jnp.zeros((kv_count, GROUP * rows), jnp.float32),
    )
    keys_all = lax.all_gather(rk, "seq", axis=0, tiled=True)
    values_all = lax.all_gather(vb, "seq", axis=0, tiled=True)
    count = keys_all.shape[0]
    block = 1024
    steps_total = count // block

    def compute(offset_blk, state):
        numer, denom = state
        keys_blk = lax.dynamic_slice_in_dim(keys_all, offset_blk, block, 0).reshape(
            block, kv_count, HD
        )
        values_blk = lax.dynamic_slice_in_dim(values_all, offset_blk, block, 0).reshape(
            block, kv_count, HD
        )
        key_index = (offset_blk + jnp.arange(block, dtype=jnp.int32)).astype(jnp.float32)
        scores = jnp.einsum("cqd,kcd->cqk", stacked, keys_blk, preferred_element_type=jnp.float32)
        capped = CAP * jnp.tanh(scores / CAP)
        allowed = (key_index[None, None, :] >= query_start[None, :, None]) & (
            key_index[None, None, :] <= query_index[None, :, None]
        )
        weights = jnp.where(allowed, jnp.exp(capped), 0.0)
        numer = numer + jnp.einsum(
            "cqk,kcd->cqd",
            weights.astype(jnp.bfloat16),
            values_blk,
            preferred_element_type=jnp.float32,
        )
        denom = denom + jnp.sum(weights, axis=2)
        return (numer, denom)

    def one_block(step, state):
        offset_blk = step * block
        return compute(offset_blk, state)

    numer, denom = lax.fori_loop(0, steps_total, one_block, empty)
    attn = (numer / denom[:, :, None]).reshape(kv_count, GROUP, rows, HD).transpose(2, 0, 1, 3)
    attn = attn.reshape(rows, kv_count * GROUP * HD).astype(jnp.bfloat16)
    partial_proj = jnp.dot(
        attn, lax.all_gather(w_out, "seq", axis=1, tiled=True), preferred_element_type=jnp.float32
    )
    partial_proj = lax.optimization_barrier(partial_proj.astype(jnp.bfloat16)).astype(jnp.float32)
    summed = lax.psum(partial_proj.astype(jnp.bfloat16), "head").astype(jnp.float32)
    scale = lax.rsqrt(jnp.mean(summed * summed, axis=1, keepdims=True) + EPS)
    return (wide + summed * scale * post_gain).astype(jnp.bfloat16)


def solution(mesh):
    return jax.shard_map(
        local,
        mesh=mesh,
        in_specs=(
            P("seq", "head"),
            P("seq"),
            P(),
            P(),
            P("seq", "head"),
            P("seq", "head"),
            P("seq", "head"),
            P("head", "seq"),
        ),
        out_specs=P("seq", None),
        check_vma=False,
    )
```

profile of v0, /device:TPU:0, one launch (start us, length us, event | category | flops | bytes accessed | tf_op | source)
XLA Modules:
  0.0 300.0 jit_solution(1061354986700771852)
XLA Ops:
  6.5 0.7 all-gather.8.cloned.1.call-update
  7.3 0.7 all-gather.10.cloned.1.call-update
  8.1 0.7 all-gather.14.cloned.1.call-update
  10.0 0.8 convert_reduce_fusion
  10.8 1.3 dynamic-slice
  12.9 23.1 %all-reduce = f32[64]{0:T(128)S(1)} all-reduce(f32[64]{0:T(128)S(1)} %dynamic-update-slice), channel_id=2, replica_groups=mesh['seq'=8,'head'=4] {'seq'}, use_global_device_ids=true, to_apply=%add | all-reduce | flops 64 | bytes 512
  36.4 0.8 select_reduce_fusion
  37.5 2.4 fusion.14
  39.9 39.1 %all-gather.10.cloned.1.call-done = bf16[4608,128]{1,0:T(8,128)(2,1)} async-done(((bf16[576,128]{1,0:T(8,128)(2,1)}), bf16[4608,128]{1,0:T(8,128)(2,1)}) %all-gather.10.cloned.1.call-update) | async-done | bytes 1179664 | tf_op jit(solution)/shard_map/all_gather | solution.py:55
  79.0 2.3 convolution_bitcast_fusion.1
  81.7 34.4 %all-gather.1 = bf16[2048,1,128]{0,2,1:T(8,128)(2,1)} all-gather(bf16[256,1,128]{0,2,1:T(8,128)(2,1)S(1)} %pad_maximum_fusion), channel_id=3, replica_groups=mesh['seq'=8,'head'=4] {'seq'}, dimensions={0}, use_global_device_ids=true | all-gather | bytes 589824 | tf_op jit(solution)/shard_map/all_gather | solution.py:85
  116.1 6.3 %all-gather.14.cloned.1.call-done = bf16[4608,128]{1,0:T(8,128)(2,1)} async-done(((bf16[576,128]{1,0:T(8,128)(2,1)}), bf16[4608,128]{1,0:T(8,128)(2,1)}) %all-gather.14.cloned.1.call-update) | async-done | bytes 1179664 | tf_op jit(solution)/shard_map/all_gather | solution.py:56
  122.4 2.2 convolution_convert_fusion.1
  124.6 32.3 %all_gather.34 = bf16[2048,128]{1,0:T(8,128)(2,1)S(1)} all-gather(bf16[256,128]{1,0:T(8,128)(2,1)S(1)} %convolution_convert_fusion.1), channel_id=1, replica_groups=mesh['seq'=8,'head'=4] {'seq'}, dimensions={0}, use_global_device_ids=true | all-gather | bytes 589824 | tf_op jit(solution)/shard_map/all_gather | solution.py:86
  156.9 20.0 %all-gather.12.cloned.1.call-done = bf16[4608,256]{1,0:T(8,128)(2,1)} async-done(((bf16[576,256]{1,0:T(8,128)(2,1)}), bf16[4608,256]{1,0:T(8,128)(2,1)}) %all-gather.12.cloned.1.call-update) | async-done | bytes 2359312 | tf_op jit(solution)/shard_map/all_gather | solution.py:54
  177.0 3.0 fusion.30
  180.1 5.0 %while.31 = (s32[]{:T(128)}, f32[1,512,128]{2,1,0:T(8,128)S(1)}, f32[1,512]{1,0:T(1,128)S(1)}, bf16[2048,128]{0,1:T(8,128)(2,1)}, bf16[1,512,128]{2,1,0:T(8,128)...) while((s32[]{:T(128)}, f32[1,512,128]{2,1,0:T(8,128)S(1)}, ...), condition=%wide.region_7.8_spmd.clone, body=%wide.region_5.7_spmd.clone.sunk | while | flops 272763392 | bytes 3311802 | solution.py:119
  180.2 1.9 fusion.47
  182.7 1.9 fusion.47
  185.4 44.5 %all-gather.16.cloned.1.call-done = bf16[256,4608]{0,1:T(8,128)(2,1)} async-done(((bf16[256,576]{0,1:T(8,128)(2,1)}), bf16[256,4608]{0,1:T(8,128)(2,1)}) %all-gather.16.cloned.1.call-update) | async-done | bytes 2359312 | tf_op jit(solution)/shard_map/all_gather | solution.py:123
  229.9 3.9 %convolution_convert_fusion = bf16[256,4608]{1,0:T(8,128)(2,1)} fusion(bf16[256,256]{0,1:T(8,128)(2,1)S(1)} %bitcast.59, bf16[256,4608]{0,1:T(8,128)(2,1)} %all-gather.16.cloned.1.call-done), kind=kOutput, calls=%fused_computation.21 | convolution fusion | flops 605159424 | bytes 4849664 | tf_op jit(solution)/shard_map/dot_general | solution.py:122
  233.9 54.4 %all-reduce.3.cloned.1.call-done = bf16[256,4608]{1,0:T(8,128)(2,1)} async-done(((bf16[256,4608]{1,0:T(8,128)(2,1)}), bf16[256,4608]{1,0:T(8,128)(2,1)}) %all-reduce.3.cloned.1.call-update) | async-done | bytes 2359312 | tf_op jit(solution)/shard_map/psum | solution.py:126
  288.2 2.4 fusion.12
  290.6 2.6 fusion.17
  (60 shorter events, 4.2 us)
Async XLA Ops:
  6.5 72.5 %copy-start.4 = (f32[4608]{0:T(1024)S(1)}, f32[4608]{0:T(1024)}, u32[]{:S(2)}) copy-start(f32[4608]{0:T(1024)} %param.14) | copy-start | bytes 55300
  6.5 31.0 %all-gather.8.cloned.1.call-start = ((), (), s32[]{:S(2)}) async-start(), calls=%async_computation | async-start | bytes 2949120 | tf_op jit(solution)/shard_map/all_gather | solution.py:48
  7.3 71.8 %all-gather.10.cloned.1.call-start = ((), (), s32[]{:S(2)}) async-start(), calls=%async_computation.1 | async-start | bytes 1327104 | tf_op jit(solution)/shard_map/all_gather | solution.py:55
  8.0 114.4 %all-gather.14.cloned.1.call-start = ((), (), s32[]{:S(2)}) async-start(), calls=%async_computation.3 | async-start | bytes 1327104 | tf_op jit(solution)/shard_map/all_gather | solution.py:56
  8.7 168.2 %all-gather.12.cloned.1.call-start = ((), (), s32[]{:S(2)}) async-start(), calls=%async_computation.2 | async-start | bytes 2654208 | tf_op jit(solution)/shard_map/all_gather | solution.py:54
  9.3 220.6 %all-gather.16.cloned.1.call-start = ((), (), s32[]{:S(2)}) async-start(), calls=%async_computation.4 | async-start | bytes 2654208 | tf_op jit(solution)/shard_map/all_gather | solution.py:123
  9.9 278.3 %all-reduce.3.cloned.1.call-start = ((), (), s32[]{:S(2)}) async-start(), calls=%async_computation.5 | async-start | bytes 4718592 | tf_op jit(solution)/shard_map/psum | solution.py:126
  37.5 41.5 %copy-start = (bf16[256,4608]{1,0:T(8,128)(2,1)S(1)}, bf16[256,4608]{1,0:T(8,128)(2,1)}, u32[]{:S(2)}) copy-start(bf16[256,4608]{1,0:T(8,128)(2,1)} %all-gather.8.cloned.1.call-done) | copy-start | bytes 7077892
  229.9 60.7 %copy-start.3 = (f32[4608]{0:T(1024)S(1)}, f32[4608]{0:T(1024)}, u32[]{:S(2)}) copy-start(f32[4608]{0:T(1024)} %param.15) | copy-start | bytes 55300
  233.9 56.8 %copy-start.1 = (bf16[256,4608]{1,0:T(8,128)(2,1)S(1)}, bf16[256,4608]{1,0:T(8,128)(2,1)}, u32[]{:S(2)}) copy-start(bf16[256,4608]{1,0:T(8,128)(2,1)} %all-gather.8.cloned.1.call-done) | copy-start | bytes 7077892
  288.2 2.4 copy-start.2
Sparse Core Ops, SparseCore 0:
  8.9 26.7 all-gather.7
  37.9 41.1 all-gather.9
  81.2 41.1 all-gather.13
  124.5 52.4 all-gather.11
  179.0 50.8 all-gather.15
  234.0 54.1 all-reduce.2
where the time goes:
time: 300 us
  waiting for transfers between devices  168 us (56%)
  blocking collectives  89.8 us (30%)
  matrix products  16.3 us (5%)
  between operations  14.3 us (5%)
  other arithmetic  9.87 us (3%)
    psum x1, waiting for transfers between devices, local(): lax.psum(partial_proj.astype(jnp.bfloat16), 'head').astype(jnp.float32)  54.4 us
    all_gather x1, waiting for transfers between devices, local(): lax.all_gather(w_out, 'seq', axis=1, tiled=True)  44.5 us
    all_gather x1, waiting for transfers between devices, local(): lax.all_gather(w_key, 'seq', axis=0, tiled=True)  39.1 us
    all_gather x1, blocking collectives, local(): keys_all = lax.all_gather(rk, 'seq', axis=0, tiled=True)  34.4 us
    all_gather x1, blocking collectives, local(): values_all = lax.all_gather(vb, 'seq', axis=0, tiled=True)  32.3 us
    unnamed x1, blocking collectives  23.1 us
    all_gather x1, waiting for transfers between devices, local(): lax.all_gather(w_query, 'seq', axis=0, tiled=True)  20 us
    dot_general x3, matrix products, local(): jnp.dot(normed, piece, preferred_element_type=jnp.float32)  7.5 us
  transfers between devices with their start and end apart: 6, of which 5 were waited for; matrix products, arithmetic and copies ran while one was open for 6% of the time, Pallas kernels for 0%

commit v1 on v0

--- a/solution.py
+++ b/solution.py
@@ -123,7 +123,9 @@
         attn, lax.all_gather(w_out, "seq", axis=1, tiled=True), preferred_element_type=jnp.float32
     )
     partial_proj = lax.optimization_barrier(partial_proj.astype(jnp.bfloat16)).astype(jnp.float32)
-    summed = lax.psum(partial_proj.astype(jnp.bfloat16), "head").astype(jnp.float32)
+    summed = jnp.sum(lax.all_gather(partial_proj.astype(jnp.bfloat16), "head"), axis=0).astype(
+        jnp.float32
+    )
     scale = lax.rsqrt(jnp.mean(summed * summed, axis=1, keepdims=True) + EPS)
     return (wide + summed * scale * post_gain).astype(jnp.bfloat16)
 

time: 300 us -> 315 us (1.050)
  waiting for transfers between devices: 168 us -> 176 us
  other arithmetic: 9.87 us -> 14.5 us
    all_gather x0 -> x1, waiting for transfers between devices: none -> 62.9 us  [local(): lax.all_gather(partial_proj.astype(jnp.bfloat16), 'head')]
    psum x1 -> x0, waiting for transfers between devices: 54.4 us -> none  [local(): lax.psum(partial_proj.astype(jnp.bfloat16), 'head').astype(jnp.float32)]
    reduce_sum x0 -> x1, other arithmetic: none -> 6.49 us  [local(): jnp.sum(lax.all_gather(partial_proj.astype(jnp.bfloat16), 'head'), axis=0)]
where the time goes in v1:
time: 315 us; the launch traced here: 314 us
  waiting for transfers between devices  176 us (56%)
  blocking collectives  90 us (29%)
  matrix products  16.2 us (5%)
  other arithmetic  14.5 us (5%)
  between operations  14.3 us (5%)
    all_gather x1, waiting for transfers between devices, local(): lax.all_gather(partial_proj.astype(jnp.bfloat16), 'head')  62.9 us
    all_gather x1, waiting for transfers between devices, local(): lax.all_gather(w_out, 'seq', axis=1, tiled=True)  44.5 us
    all_gather x1, waiting for transfers between devices, local(): lax.all_gather(w_key, 'seq', axis=0, tiled=True)  39.1 us
    all_gather x1, blocking collectives, local(): keys_all = lax.all_gather(rk, 'seq', axis=0, tiled=True)  34.4 us
    all_gather x1, blocking collectives, local(): values_all = lax.all_gather(vb, 'seq', axis=0, tiled=True)  32.5 us
    unnamed x1, blocking collectives  23.1 us
    all_gather x1, waiting for transfers between devices, local(): lax.all_gather(w_query, 'seq', axis=0, tiled=True)  19.7 us
    dot_general x3, matrix products, local(): jnp.dot(normed, piece, preferred_element_type=jnp.float32)  7.49 us
  transfers between devices with their start and end apart: 6, of which 5 were waited for; matrix products, arithmetic and copies ran while one was open for 6% of the time, Pallas kernels for 0%

profile of v1, /device:TPU:0, one launch (start us, length us, event | category | flops | bytes accessed | tf_op | source)
XLA Modules:
  0.0 314.1 jit_solution(405740567154756640)
XLA Ops:
  6.5 0.7 all-gather.10.cloned.1.call-update
  7.3 0.7 all-gather.12.cloned.1.call-update
  10.0 0.8 convert_reduce_fusion
  10.8 1.2 dynamic-slice
  12.9 23.1 %all-reduce = f32[64]{0:T(128)S(1)} all-reduce(f32[64]{0:T(128)S(1)} %dynamic-update-slice), channel_id=2, replica_groups=mesh['seq'=8,'head'=4] {'seq'}, use_global_device_ids=true, to_apply=%add | all-reduce | flops 64 | bytes 512
  36.4 0.8 select_reduce_fusion
  37.5 2.4 fusion.14
  39.9 39.1 %all-gather.12.cloned.1.call-done = bf16[4608,128]{1,0:T(8,128)(2,1)} async-done(((bf16[576,128]{1,0:T(8,128)(2,1)}), bf16[4608,128]{1,0:T(8,128)(2,1)}) %all-gather.12.cloned.1.call-update) | async-done | bytes 1179664 | tf_op jit(solution)/shard_map/all_gather | solution.py:55
  79.0 2.3 convolution_bitcast_fusion.1
  81.7 34.4 %all-gather.1 = bf16[2048,1,128]{0,2,1:T(8,128)(2,1)} all-gather(bf16[256,1,128]{0,2,1:T(8,128)(2,1)S(1)} %pad_maximum_fusion), channel_id=3, replica_groups=mesh['seq'=8,'head'=4] {'seq'}, dimensions={0}, use_global_device_ids=true | all-gather | bytes 589824 | tf_op jit(solution)/shard_map/all_gather | solution.py:85
  116.1 6.3 %all-gather.16.cloned.1.call-done = bf16[4608,128]{1,0:T(8,128)(2,1)} async-done(((bf16[576,128]{1,0:T(8,128)(2,1)}), bf16[4608,128]{1,0:T(8,128)(2,1)}) %all-gather.16.cloned.1.call-update) | async-done | bytes 1179664 | tf_op jit(solution)/shard_map/all_gather | solution.py:56
  122.4 2.2 convolution_convert_fusion.1
  124.6 32.5 %all_gather.40 = bf16[2048,128]{1,0:T(8,128)(2,1)S(1)} all-gather(bf16[256,128]{1,0:T(8,128)(2,1)S(1)} %convolution_convert_fusion.1), channel_id=1, replica_groups=mesh['seq'=8,'head'=4] {'seq'}, dimensions={0}, use_global_device_ids=true | all-gather | bytes 589824 | tf_op jit(solution)/shard_map/all_gather | solution.py:86
  157.1 19.7 %all-gather.14.cloned.1.call-done = bf16[4608,256]{1,0:T(8,128)(2,1)} async-done(((bf16[576,256]{1,0:T(8,128)(2,1)}), bf16[4608,256]{1,0:T(8,128)(2,1)}) %all-gather.14.cloned.1.call-update) | async-done | bytes 2359312 | tf_op jit(solution)/shard_map/all_gather | solution.py:54
  176.8 3.0 fusion.30
  180.0 5.0 %while.31 = (s32[]{:T(128)}, f32[1,512,128]{2,1,0:T(8,128)S(1)}, f32[1,512]{1,0:T(1,128)S(1)}, bf16[2048,128]{0,1:T(8,128)(2,1)}, bf16[1,512,128]{2,1,0:T(8,128)...) while((s32[]{:T(128)}, f32[1,512,128]{2,1,0:T(8,128)S(1)}, ...), condition=%wide.region_7.8_spmd.clone, body=%wide.region_5.7_spmd.clone.sunk | while | flops 272763392 | bytes 3311810 | solution.py:119
  180.1 1.9 fusion.47
  182.6 1.9 fusion.47
  185.3 44.5 %all-gather.18.cloned.1.call-done = bf16[256,4608]{0,1:T(8,128)(2,1)} async-done(((bf16[256,576]{0,1:T(8,128)(2,1)}), bf16[256,4608]{0,1:T(8,128)(2,1)}) %all-gather.18.cloned.1.call-update) | async-done | bytes 2359312 | tf_op jit(solution)/shard_map/all_gather | solution.py:123
  229.8 3.9 %convolution_convert_fusion = bf16[256,4608]{1,0:T(8,128)(2,1)} fusion(bf16[256,256]{0,1:T(8,128)(2,1)S(1)} %bitcast.61, bf16[256,4608]{0,1:T(8,128)(2,1)} %all-gather.18.cloned.1.call-done), kind=kOutput, calls=%fused_computation.21 | convolution fusion | flops 605159424 | bytes 4849664 | tf_op jit(solution)/shard_map/dot_general | solution.py:122
  233.7 62.9 %all-gather.20.cloned.1.call-done = bf16[1024,4608]{1,0:T(8,128)(2,1)} async-done(((bf16[256,4608]{1,0:T(8,128)(2,1)}), bf16[1024,4608]{1,0:T(8,128)(2,1)}) %all-gather.20.cloned.1.call-update) | async-done | bytes 9437200 | tf_op jit(solution)/shard_map/all_gather | solution.py:126
  296.6 6.5 %reduce_sum.64 = bf16[256,4608]{1,0:T(8,128)(2,1)S(1)} reduce(bf16[4,256,4608]{2,1,0:T(8,128)(2,1)} %bitcast.60, bf16[]{:T(256)} %constant.96.clone.1), dimensions={0}, to_apply=%region_8.9 | reduce | flops 3538944 | bytes 11796482 | tf_op jit(solution)/shard_map/reduce_sum | solution.py:126
  303.7 1.1 copy-done.1
  304.8 2.5 fusion.17
  (59 shorter events, 5.4 us)
Async XLA Ops:
  6.5 72.5 %copy-start.3 = (f32[4608]{0:T(1024)S(1)}, f32[4608]{0:T(1024)}, u32[]{:S(2)}) copy-start(f32[4608]{0:T(1024)} %param.14) | copy-start | bytes 55300
  6.5 31.0 %all-gather.10.cloned.1.call-start = ((), (), s32[]{:S(2)}) async-start(), calls=%async_computation | async-start | bytes 2949120 | tf_op jit(solution)/shard_map/all_gather | solution.py:48
  7.3 71.8 %all-gather.12.cloned.1.call-start = ((), (), s32[]{:S(2)}) async-start(), calls=%async_computation.1 | async-start | bytes 1327104 | tf_op jit(solution)/shard_map/all_gather | solution.py:55
  8.0 114.4 %all-gather.16.cloned.1.call-start = ((), (), s32[]{:S(2)}) async-start(), calls=%async_computation.3 | async-start | bytes 1327104 | tf_op jit(solution)/shard_map/all_gather | solution.py:56
  8.7 168.1 %all-gather.14.cloned.1.call-start = ((), (), s32[]{:S(2)}) async-start(), calls=%async_computation.2 | async-start | bytes 2654208 | tf_op jit(solution)/shard_map/all_gather | solution.py:54
  9.3 220.5 %all-gather.18.cloned.1.call-start = ((), (), s32[]{:S(2)}) async-start(), calls=%async_computation.4 | async-start | bytes 2654208 | tf_op jit(solution)/shard_map/all_gather | solution.py:123
  9.9 286.7 %all-gather.20.cloned.1.call-start = ((), (), s32[]{:S(2)}) async-start(), calls=%async_computation.5 | async-start | bytes 11796480 | tf_op jit(solution)/shard_map/all_gather | solution.py:126
  37.5 41.5 %copy-start = (bf16[256,4608]{1,0:T(8,128)(2,1)S(1)}, bf16[256,4608]{1,0:T(8,128)(2,1)}, u32[]{:S(2)}) copy-start(bf16[256,4608]{1,0:T(8,128)(2,1)} %all-gather.10.cloned.1.call-done) | copy-start | bytes 7077892
  296.6 7.1 %copy-start.2 = (f32[4608]{0:T(1024)S(1)}, f32[4608]{0:T(1024)}, u32[]{:S(2)}) copy-start(f32[4608]{0:T(1024)} %param.15) | copy-start | bytes 55300
  303.1 1.7 copy-start.1
Sparse Core Ops, SparseCore 0:
  8.9 26.7 all-gather.9
  37.9 41.1 all-gather.11
  81.2 41.1 all-gather.15
  124.4 52.3 all-gather.13
  178.9 50.8 all-gather.17
  233.8 62.7 all-gather.19
